TPU v7x, 32 devices: a whole 2x2x4 slice. The times are simulated.
32 devices in a mesh: dp: 8 (over z, x), mp: 4 (over y, core).
Axes of the slice: x: 2, y: 2, z: 4, core: 2. Of those that a mesh axis runs over, the one named last changes fastest.
Arguments:
- text_in: bfloat16 [7680, 768], P(('dp', 'mp')), may hold values from -6 to 6
- caption_ids: int32 [480, 16], P('dp'), may hold values from 0 to 31999, as said below
- pairing: int32 [480], replicated, may hold values from 0 to 479, each once
- image_low: bfloat16 [19200, 768], P(('dp', 'mp')), may hold values from -6 to 6
- image_high: bfloat16 [13920, 768], P(('dp', 'mp')), may hold values from -6 to 6
- img_gains: float32 [2, 768], replicated, may hold values from 0.5 to 1.5
- img_qkv: bfloat16 [3, 768, 768], P(None, None, 'mp'), may hold values from -0.21875 to 0.21875
- img_out: bfloat16 [768, 768], P('mp'), may hold values from -0.625 to 0.625
- img_fc1: bfloat16 [768, 3072], P(None, 'mp'), may hold values from -0.21875 to 0.21875
- img_fc2: bfloat16 [3072, 768], P('mp'), may hold values from -0.109375 to 0.109375
- txt_qkv: bfloat16 [3, 768, 768], P(None, None, 'mp'), may hold values from -0.21875 to 0.21875
- txt_qv_bias: float32 [2, 768], P(None, 'mp'), may hold values from -3 to 3
- txt_out: bfloat16 [768, 768], P('mp'), may hold values from -0.4375 to 0.4375
- txt_fc1: bfloat16 [768, 3072], P(None, 'mp'), may hold values from -0.21875 to 0.21875
- txt_fc1_bias: float32 [3072], P('mp'), may hold values from -3 to 3
- txt_fc2: bfloat16 [3072, 768], P('mp'), may hold values from -0.109375 to 0.109375
- txt_gains: float32 [2, 768], replicated, may hold values from 0.5 to 1.5
- txt_shifts: float32 [2, 768], replicated, may hold values from -2 to 2
- txt_biases: float32 [2, 768], replicated, may hold values from -2 to 2
Outputs:
- loss: float32 [], replicated
- grad_text_in: float32 [7680, 768], P(('dp', 'mp'))
- grad_qkv: float32 [3, 768, 768], P(None, None, 'mp')
- grad_qv_bias: float32 [2, 768], P(None, 'mp')
- grad_out: float32 [768, 768], P('mp')
- grad_fc1: float32 [768, 3072], P(None, 'mp')
- grad_fc1_bias: float32 [3072], P('mp')
- grad_fc2: float32 [3072, 768], P('mp')
- grad_gains: float32 [2, 768], replicated
- grad_shifts: float32 [2, 768], replicated
- grad_biases: float32 [2, 768], replicated
Inputs may be any that keep to these rules, and one draw needn't show every extreme that they name: `caption_ids`: in each caption the nonzero ids come first and the zeros after; each caption has 4 to 16 nonzero ids. Image i is paired with caption pairing[i]; each caption is paired once.
All inputs are finite; a program needn't handle non-finite values.
Results may differ from a plain program's by a relative error of at most 0.017.
Values may be sent and summed in bfloat16 or wider, within the bound.
A program may use at most 192 MiB of HBM per device.

v0:
```python
import jax
import jax.numpy as jnp
from jax import lax
from jax.sharding import PartitionSpec as P

D = 768
HEAD = 64
L = 16
P_LOW = 50
P_HIGH = 145
EPS = 1e-06
SCALE = 40.0
LOSS_SCALE = 16.0
MASKED = -1e30


def layer_stats(values):
    center = values - jnp.mean(values, -1, keepdims=True)
    inverse = lax.rsqrt(jnp.mean(center * center, -1, keepdims=True) + EPS)
    return (center * inverse, inverse)


def norm_back(grad_out, unit, inverse, gain):
    scaled = grad_out * gain
    return inverse * (
        scaled
        - jnp.mean(scaled, -1, keepdims=True)
        - unit * jnp.mean(scaled * unit, -1, keepdims=True)
    )


def gelu_exact(values):
    return jax.nn.gelu(values, approximate=False)


def score_rows(queries, keys_all, keep):
    scores = (
        jnp.einsum("nqhe,nkhe->nhqk", queries, keys_all, preferred_element_type=jnp.float32) * 0.125
    )
    if keep is not None:
        scores = jnp.where(keep, scores, MASKED)
    return scores


def attention_shares(queries, keys_all, keep):
    scores = score_rows(queries, keys_all, keep)
    highest = jnp.max(scores, -1, keepdims=True)
    raised = jnp.exp(scores - highest)
    totals = jnp.sum(raised, -1, keepdims=True)
    return (raised / totals, highest + jnp.log(totals))


def image_tower(tokens, count, length, gains, weights):
    w_qkv, w_out, w_fc1, w_fc2 = weights
    head_count = D // HEAD
    inputs = tokens.astype(jnp.float32)
    unit, spare = layer_stats(inputs)
    normed = (unit * gains[0]).astype(jnp.bfloat16)
    projected = jnp.einsum("rd,jdw->jrw", normed, w_qkv, preferred_element_type=jnp.float32).astype(
        jnp.bfloat16
    )
    shaped = projected.reshape(3, count, length, head_count, HEAD)
    shares, spare_lse = attention_shares(shaped[0], shaped[1], None)
    context = jnp.einsum(
        "nhqk,nkhe->nqhe",
        shares.astype(jnp.bfloat16),
        shaped[2],
        preferred_element_type=jnp.float32,
    )
    context = context.astype(jnp.bfloat16).reshape(count * length, D)
    middle = inputs + jnp.dot(context, w_out, preferred_element_type=jnp.float32)
    unit2, spare2 = layer_stats(middle)
    normed2 = (unit2 * gains[1]).astype(jnp.bfloat16)
    active = gelu_exact(jnp.dot(normed2, w_fc1, preferred_element_type=jnp.float32)).astype(
        jnp.bfloat16
    )
    result = middle + jnp.dot(active, w_fc2, preferred_element_type=jnp.float32)
    pooled = jnp.mean(result.reshape(count, length, D), 1)
    return (pooled * lax.rsqrt(jnp.sum(pooled * pooled, -1, keepdims=True) + EPS)).astype(
        jnp.bfloat16
    )


def local(
    text_in,
    caption_ids,
    pairing,
    image_low,
    image_high,
    img_gains,
    img_qkv,
    img_out,
    img_fc1,
    img_fc2,
    txt_qkv,
    txt_qv_bias,
    txt_out,
    txt_fc1,
    txt_fc1_bias,
    txt_fc2,
    txt_gains,
    txt_shifts,
    txt_biases,
):
    weights = (
        lax.all_gather(img_qkv, "mp", axis=2, tiled=True),
        lax.all_gather(img_out, "mp", axis=0, tiled=True),
        lax.all_gather(img_fc1, "mp", axis=1, tiled=True),
        lax.all_gather(img_fc2, "mp", axis=0, tiled=True),
    )
    low_count = image_low.shape[0] // P_LOW
    high_count = image_high.shape[0] // P_HIGH
    images16 = jnp.concatenate(
        [
            image_tower(image_low, low_count, P_LOW, img_gains, weights),
            image_tower(image_high, high_count, P_HIGH, img_gains, weights),
        ],
        0,
    )
    width = txt_qkv.shape[2]
    head_count = width // HEAD
    own_rows = text_in.shape[0]
    own_caps = own_rows // L
    group_caps = caption_ids.shape[0]
    group_rows = group_caps * L
    own_ids = lax.dynamic_slice_in_dim(caption_ids, lax.axis_index("mp") * own_caps, own_caps, 0)
    keep = (caption_ids > 0)[:, None, None, :]
    inputs = text_in.astype(jnp.float32)
    unit1, inverse1 = layer_stats(inputs)
    normed1 = (unit1 * txt_gains[0] + txt_shifts[0]).astype(jnp.bfloat16)
    bias_rows = jnp.stack([txt_qv_bias[0], jnp.zeros_like(txt_qv_bias[0]), txt_qv_bias[1]])
    piece = lax.all_gather(normed1, "mp", axis=0, tiled=True)
    made = jnp.einsum("rd,jdw->rjw", piece, txt_qkv, preferred_element_type=jnp.float32) + bias_rows
    joined = jnp.concatenate(
        [piece, made.astype(jnp.bfloat16).reshape(piece.shape[0], 3 * width)], 1
    )
    normed1_all = joined[:, :D]
    triple = joined[:, D:].reshape(group_caps, L, 3, head_count, HEAD)
    queries = triple[:, :, 0]
    keys_all = triple[:, :, 1]
    values_all = triple[:, :, 2]
    shares, log_totals = attention_shares(queries, keys_all, keep)
    context = jnp.einsum(
        "nhqk,nkhe->nqhe",
        shares.astype(jnp.bfloat16),
        values_all,
        preferred_element_type=jnp.float32,
    )
    context = context.astype(jnp.bfloat16).reshape(group_rows, width)
    middle = inputs + (
        lax.psum_scatter(
            jnp.dot(context, txt_out, preferred_element_type=jnp.float32).astype(jnp.bfloat16),
            "mp",
            scatter_dimension=0,
            tiled=True,
        ).astype(jnp.float32)
        + txt_biases[0]
    )
    unit2, inverse2 = layer_stats(middle)
    normed2 = (unit2 * txt_gains[1] + txt_shifts[1]).astype(jnp.bfloat16)
    piece = lax.all_gather(normed2, "mp", axis=0, tiled=True)
    hidden_piece = jnp.dot(piece, txt_fc1, preferred_element_type=jnp.float32) + txt_fc1_bias
    spread = jnp.concatenate([piece.astype(jnp.float32), hidden_piece], 1)
    normed2_all = spread[:, :D].astype(jnp.bfloat16)
    hidden = spread[:, D:]
    active, gelu_pull = jax.vjp(gelu_exact, hidden)
    active16 = active.astype(jnp.bfloat16)
    result = middle + (
        lax.psum_scatter(
            jnp.dot(active16, txt_fc2, preferred_element_type=jnp.float32).astype(jnp.bfloat16),
            "mp",
            scatter_dimension=0,
            tiled=True,
        ).astype(jnp.float32)
        + txt_biases[1]
    )
    present = (own_ids > 0).astype(jnp.float32)
    counts = jnp.sum(present, 1, keepdims=True)
    pooled = jnp.sum(result.reshape(own_caps, L, D) * present[:, :, None], 1) / counts
    inverse_len = lax.rsqrt(jnp.sum(pooled * pooled, -1, keepdims=True) + EPS)
    captions_unit = pooled * inverse_len
    captions16 = captions_unit.astype(jnp.bfloat16)
    total_pairs = pairing.shape[0]
    first_pair = lax.axis_index(("dp", "mp")) * own_caps
    arrived = lax.all_gather(captions16, ("dp", "mp"), axis=0, tiled=True)
    logits = SCALE * jnp.einsum("id,jd->ij", images16, arrived, preferred_element_type=jnp.float32)
    targets = lax.dynamic_slice_in_dim(pairing, first_pair, own_caps, 0)
    matched = (targets[:, None] == jnp.arange(total_pairs)[None, :]).astype(jnp.float32)
    raised = jnp.exp(logits - SCALE)
    local_lse = SCALE + jnp.log(jnp.sum(raised, 1))
    partial_value = jnp.sum(raised, 0)
    own_term = 0.5 * jnp.sum(local_lse) - jnp.sum(matched * logits)
    summed, scalar = lax.psum((partial_value, own_term), ("dp", "mp"))
    other_lse = SCALE + jnp.log(summed)
    total = scalar + 0.5 * jnp.sum(other_lse)
    loss = total / total_pairs
    grads16 = (
        LOSS_SCALE
        * (
            0.5 * jnp.exp(logits - local_lse[:, None])
            + 0.5 * jnp.exp(logits - other_lse[None, :])
            - matched
        )
    ).astype(jnp.bfloat16)
    grad_caps = lax.psum_scatter(
        SCALE * jnp.einsum("ic,id->cd", grads16, images16, preferred_element_type=jnp.float32),
        ("dp", "mp"),
        scatter_dimension=0,
        tiled=True,
    )
    grad_pooled = inverse_len * (
        grad_caps - captions_unit * jnp.sum(captions_unit * grad_caps, -1, keepdims=True)
    )
    grad_result = (grad_pooled[:, None, :] * (present / counts)[:, :, None]).reshape(own_rows, D)
    grad_all = lax.all_gather(grad_result.astype(jnp.bfloat16), "mp", axis=0, tiled=True)
    grad_fc2 = jnp.einsum("gf,gd->fd", active16, grad_all, preferred_element_type=jnp.float32)
    grad_active = jnp.einsum("gd,fd->gf", grad_all, txt_fc2, preferred_element_type=jnp.float32)
    grad_hidden16 = gelu_pull(grad_active)[0].astype(jnp.bfloat16)
    grad_fc1 = jnp.einsum(
        "gd,gf->df", normed2_all, grad_hidden16, preferred_element_type=jnp.float32
    )
    grad_fc1_bias = jnp.sum(grad_hidden16.astype(jnp.float32), 0)
    grad_normed2 = lax.psum_scatter(
        jnp.einsum("gf,df->gd", grad_hidden16, txt_fc1, preferred_element_type=jnp.float32).astype(
            jnp.bfloat16
        ),
        "mp",
        scatter_dimension=0,
        tiled=True,
    ).astype(jnp.float32)
    grad_middle = grad_result + norm_back(grad_normed2, unit2, inverse2, txt_gains[1])
    grad_mid_all = lax.all_gather(grad_middle.astype(jnp.bfloat16), "mp", axis=0, tiled=True)
    grad_out = jnp.einsum("gw,gd->wd", context, grad_mid_all, preferred_element_type=jnp.float32)
    grad_context = jnp.einsum(
        "gd,wd->gw", grad_mid_all, txt_out, preferred_element_type=jnp.float32
    )
    grad_context = grad_context.astype(jnp.bfloat16).reshape(group_caps, L, head_count, HEAD)
    shares_again = jnp.exp(score_rows(queries, keys_all, keep) - log_totals)
    grad_shares = jnp.einsum(
        "nqhe,nkhe->nhqk", grad_context, values_all, preferred_element_type=jnp.float32
    )
    grad_values = jnp.einsum(
        "nhqk,nqhe->nkhe",
        shares_again.astype(jnp.bfloat16),
        grad_context,
        preferred_element_type=jnp.float32,
    ).astype(jnp.bfloat16)
    grad_scores = (
        shares_again * (grad_shares - jnp.sum(grad_shares * shares_again, -1, keepdims=True))
    ).astype(jnp.bfloat16)
    grad_queries = (
        jnp.einsum("nhqk,nkhe->nqhe", grad_scores, keys_all, preferred_element_type=jnp.float32)
        * 0.125
    ).astype(jnp.bfloat16)
    grad_keys = (
        jnp.einsum("nhqk,nqhe->nkhe", grad_scores, queries, preferred_element_type=jnp.float32)
        * 0.125
    ).astype(jnp.bfloat16)
    grad_triple = jnp.stack([grad_queries, grad_keys, grad_values], 0).reshape(3, group_rows, width)
    grad_qkv = jnp.einsum(
        "gd,jgw->jdw", normed1_all, grad_triple, preferred_element_type=jnp.float32
    )
    grad_qv_bias = jnp.stack(
        [
            jnp.sum(grad_triple[0].astype(jnp.float32), 0),
            jnp.sum(grad_triple[2].astype(jnp.float32), 0),
        ]
    )
    grad_normed1 = lax.psum_scatter(
        jnp.einsum("jgw,jdw->gd", grad_triple, txt_qkv, preferred_element_type=jnp.float32).astype(
            jnp.bfloat16
        ),
        "mp",
        scatter_dimension=0,
        tiled=True,
    ).astype(jnp.float32)
    grad_inputs = grad_middle + norm_back(grad_normed1, unit1, inverse1, txt_gains[0])
    summed_grads = lax.psum(
        (grad_qkv, grad_qv_bias, grad_out, grad_fc1, grad_fc1_bias, grad_fc2), "dp"
    )
    small_parts = jnp.stack(
        [
            jnp.sum(grad_normed1 * unit1, 0),
            jnp.sum(grad_normed2 * unit2, 0),
            jnp.sum(grad_normed1, 0),
            jnp.sum(grad_normed2, 0),
            jnp.sum(grad_middle, 0),
            jnp.sum(grad_result, 0),
        ]
    )
    shared = lax.psum(small_parts, ("dp", "mp"))
    return (
        loss,
        grad_inputs,
        summed_grads[0],
        summed_grads[1],
        summed_grads[2],
        summed_grads[3],
        summed_grads[4],
        summed_grads[5],
        shared[0:2],
        shared[2:4],
        shared[4:6],
    )


def solution(mesh):
    placed = (
        P(("dp", "mp"), None),
        P("dp", None),
        P(),
        P(("dp", "mp"), None),
        P(("dp", "mp"), None),
        P(),
        P(None, None, "mp"),
        P("mp", None),
        P(None, "mp"),
        P("mp", None),
        P(None, None, "mp"),
        P(None, "mp"),
        P("mp", None),
        P(None, "mp"),
        P("mp"),
        P("mp", None),
        P(),
        P(),
        P(),
    )
    return jax.shard_map(
        local,
        mesh=mesh,
        in_specs=placed,
        out_specs=(
            P(),
            P(("dp", "mp"), None),
            P(None, None, "mp"),
            P(None, "mp"),
            P("mp", None),
            P(None, "mp"),
            P("mp"),
            P("mp", None),
            P(),
            P(),
            P(),
        ),
        check_vma=False,
    )
```

profile of v0, /device:TPU:0, one launch (start us, length us, event | category | flops | bytes accessed | tf_op | source)
XLA Modules:
  0.0 829.3 jit_solution(6300139161258848959)
XLA Ops:
  14.9 20.2 %all-gather.18.cloned.1.call-done = bf16[960,768]{1,0:T(8,128)(2,1)} async-done(((bf16[240,768]{1,0:T(8,128)(2,1)}), bf16[960,768]{1,0:T(8,128)(2,1)}) %all-gather.18.cloned.1.call-update) | async-done | bytes 1474576 | tf_op jit(solution)/shard_map/all_gather | solution.py:132
  40.9 3.0 reshape_reshape.3
  43.9 3.2 fusion.221
  59.0 20.6 %reduce-scatter.7.cloned.1.call-done = bf16[240,768]{1,0:T(8,128)(2,1)} async-done(((bf16[960,768]{1,0:T(8,128)(2,1)}), bf16[240,768]{1,0:T(8,128)(2,1)}) %reduce-scatter.7.cloned.1.call-update) | async-done | bytes 368656 | tf_op jit(solution)/shard_map/reduce_scatter | solution.py:151
  84.2 27.8 %all-gather.10.cloned.1.call-done = bf16[3,768,768]{1,2,0:T(8,128)(2,1)} async-done(((bf16[3,768,192]{1,2,0:T(8,128)(2,1)}), bf16[3,768,768]{1,2,0:T(8,128)(2,1)}) %all-gather.10.cloned.1.call-update) | async-done | bytes 3538960 | tf_op jit(solution)/shard_map/all_gather | solution.py:106
  112.0 4.5 convert_bitcast_fusion
  117.9 4.5 squeeze.30
  122.4 4.1 squeeze.31
  126.5 3.8 fusion.45
  130.3 3.2 fusion.229
  136.3 4.5 convert_bitcast_fusion.1
  142.7 4.2 reshape.220
  156.6 3.3 reshape.237
  162.3 3.8 fusion.227
  168.5 4.1 fusion.69
  179.6 29.0 %all-gather.16.cloned.1.call-done = bf16[3072,768]{1,0:T(8,128)(2,1)} async-done(((bf16[768,768]{1,0:T(8,128)(2,1)}), bf16[3072,768]{1,0:T(8,128)(2,1)}) %all-gather.16.cloned.1.call-update) | async-done | bytes 4718608 | tf_op jit(solution)/shard_map/all_gather | solution.py:109
  208.6 25.3 %fusion.58 = f32[600,768]{1,0:T(8,128)S(1)} fusion(f32[600,768]{1,0:T(8,128)} %copy-done.23, bf16[3072,768]{1,0:T(8,128)(2,1)} %all-gather.16.cloned.1.call-done, bf16[768,3072]{1,0:T(8,128)(2,1)} %all-gather.14.cloned.1.call-done, f32[768]{0:T(1024)S(1)} %get-tuple-element.22, f32[600]{0:T(1024)S(1)} %add_rsqrt_fusion, f32[600]{0:T(1024)S(1)} %broadcast_multiply_fusion), kind=kOutput, calls=%fused_computation.102 | convolution fusion | flops 5784422400 | bytes 13131456 | tf_op jit(solution)/shard_map/dot_general | solution.py:77
  234.0 10.1 %multiply_convert_fusion = (bf16[960,768]{1,0:T(8,128)(2,1)S(1)}, f32[960,768]{1,0:T(8,128)}, f32[960,768]{1,0:T(8,128)}) fusion(f32[768]{0:T(1024)S(1)} %copy-done.64, bf16[960,768]{1,0:T(8,128)(2,1)} %all-gather.20.cloned.1.call-done, bf16[768,768]{1,0:T(8,128)(2,1)S(1)} %copy-done), kind=kOutput, calls=%fused_computation.54 | convolution fusion | flops 1181122560 | bytes 10030080 | tf_op jit(solution)/shard_map/dot_general | solution.py:162
  248.0 20.6 %fusion.62 = f32[435,768]{1,0:T(8,128)} fusion(f32[435,768]{1,0:T(8,128)} %copy-done.25, bf16[3072,768]{1,0:T(8,128)(2,1)} %all-gather.16.cloned.1.call-done, bf16[768,3072]{1,0:T(8,128)(2,1)} %all-gather.14.cloned.1.call-done, f32[768]{0:T(1024)S(1)} %get-tuple-element.22, f32[435]{0:T(512)S(1)} %add_rsqrt_fusion.2, f32[435]{0:T(512)S(1)} %broadcast_multiply_fusion.2), kind=kOutput, calls=%fused_computation.115 | convolution fusion | flops 4193706240 | bytes 12116376 | tf_op jit(solution)/shard_map/dot_general | solution.py:77
  277.0 42.7 %all-gather = bf16[32,15,768]{2,1,0:T(8,128)(2,1)S(1)} all-gather(bf16[1,15,768]{2,1,0:T(8,128)(2,1)S(1)} %fusion.139), channel_id=1, replica_groups=mesh['dp'=8,'mp'=4] {'dp','mp'}, dimensions={0}, use_global_device_ids=true | all-gather | bytes 760320 | tf_op jit(solution)/shard_map/all_gather | solution.py:185
  321.5 36.8 %psum.64 = f32[480]{0:T(512)S(1)} all-reduce(f32[480]{0:T(512)S(1)} %get-tuple-element.19), channel_id=1, replica_groups=mesh['dp'=8,'mp'=4] {'dp','mp'}, use_global_device_ids=true, to_apply=%region_32.33 | all-reduce | flops 480 | bytes 3840 | tf_op jit(solution)/shard_map/psum | solution.py:193
  360.7 77.1 %fusion = f32[16,768]{1,0:T(8,128)S(1)} fusion(f32[480,768]{1,0:T(8,128)S(1)} %convolution_multiply_fusion), kind=kCustom, calls=%all-reduce-scatter | all-reduce-scatter fusion | flops 393217 | bytes 1523712
  445.0 18.3 %all-gather.22.cloned.1.call-done = bf16[960,768]{1,0:T(8,128)(2,1)} async-done(((bf16[240,768]{1,0:T(8,128)(2,1)}), bf16[960,768]{1,0:T(8,128)(2,1)}) %all-gather.22.cloned.1.call-update) | async-done | bytes 1474576 | tf_op jit(solution)/shard_map/all_gather | solution.py:215
  463.3 5.6 convert_reduce_fusion
  472.6 27.5 %reduce-scatter.11.cloned.1.call-done = bf16[240,768]{1,0:T(8,128)(2,1)} async-done(((bf16[960,768]{1,0:T(8,128)(2,1)}), bf16[240,768]{1,0:T(8,128)(2,1)}) %reduce-scatter.11.cloned.1.call-update) | async-done | bytes 368656 | tf_op jit(solution)/shard_map/reduce_scatter | solution.py:223
  505.8 18.1 %all-gather.24.cloned.1.call-done = bf16[960,768]{1,0:T(8,128)(2,1)} async-done(((bf16[240,768]{1,0:T(8,128)(2,1)}), bf16[960,768]{1,0:T(8,128)(2,1)}) %all-gather.24.cloned.1.call-update) | async-done | bytes 1474576 | tf_op jit(solution)/shard_map/all_gather | solution.py:232
  545.4 3.9 bitcast_convert_fusion
  549.6 4.8 fusion.234
  563.4 13.5 %reduce-scatter.13.cloned.1.call-done = bf16[240,768]{1,0:T(8,128)(2,1)} async-done(((bf16[960,768]{1,0:T(8,128)(2,1)}), bf16[240,768]{1,0:T(8,128)(2,1)}) %reduce-scatter.13.cloned.1.call-update) | async-done | bytes 368656 | tf_op jit(solution)/shard_map/reduce_scatter | solution.py:269
  578.4 23.1 %all-reduce.3 = (f32[2,192]{1,0:T(2,128)}, f32[768]{0:T(1024)}) all-reduce(f32[2,192]{1,0:T(2,128)S(1)} %pad_maximum_fusion.7, f32[768]{0:T(1024)S(1)} %get-tuple-element.38), channel_id=1, replica_groups=mesh['dp'=8,'mp'=4] {'dp'}, use_global_device_ids=true, to_apply=%region_46.47 | all-reduce | flops 1152 | bytes 9216 | tf_op jit(solution)/shard_map/psum | solution.py:278
  601.5 41.9 %all-reduce.2 = (f32[]{:T(128)}, f32[6,768]{1,0:T(8,128)S(1)}) all-reduce(f32[]{:T(128)S(6)} %sub.157, f32[6,768]{1,0:T(8,128)S(1)} %stack.59), channel_id=1, replica_groups=mesh['dp'=8,'mp'=4] {'dp','mp'}, use_global_device_ids=true, to_apply=%region_30.31 | all-reduce | flops 4609 | bytes 36872 | tf_op jit(solution)/shard_map/psum | solution.py:193
  646.8 168.1 %all-reduce.7.cloned.1.call-done = (f32[3,768,192]{1,2,0:T(8,128)}, f32[192,768]{1,0:T(8,128)}, f32[768,768]{1,0:T(8,128)}, f32[768,768]{1,0:T(8,128)}) async-done(((f32[3,768,192]{1,2,0:T(8,128)}, f32[192,768]{1,0:T(8,128)}, f32[768,768]{1,0:T(8,128)}, f32[768,768]{1,0:T(8,128)}), (f32[3,768,192]{1,2,0:T(8,128)}, f32[192,768]{1,0:T(8,128)}, f32[768,768]{1,0:T(8,128)}, ...) | async-done | bytes 7077904 | tf_op jit(solution)/shard_map/psum | solution.py:278
  (302 shorter events, 129.2 us)
Async XLA Ops:
  7.2 226.8 %copy-start = (bf16[768,768]{1,0:T(8,128)(2,1)S(1)}, bf16[768,768]{1,0:T(8,128)(2,1)}, u32[]{:S(2)}) copy-start(bf16[768,768]{1,0:T(8,128)(2,1)} %param.32) | copy-start | bytes 3538948
  7.2 27.9 %all-gather.18.cloned.1.call-start = ((), (), s32[]{:S(2)}) async-start(), calls=%async_computation.8 | async-start | bytes 1843200 | tf_op jit(solution)/shard_map/all_gather | solution.py:132
  10.5 71.6 %copy-start.43 = (f32[768]{0:T(1024)}, f32[768]{0:T(1024)S(1)}, u32[]{:S(2)}) copy-start(f32[768]{0:T(1024)S(1)} %get-tuple-element.82) | copy-start | bytes 9220
  13.1 66.5 %reduce-scatter.7.cloned.1.call-start = ((), (), s32[]{:S(2)}) async-start(), calls=%async_computation.9 | async-start | bytes 1843200 | tf_op jit(solution)/shard_map/reduce_scatter | solution.py:151
  52.1 59.9 %all-gather.10.cloned.1.call-start = ((), (), s32[]{:S(2)}) async-start(), calls=%async_computation.4 | async-start | bytes 4423680 | tf_op jit(solution)/shard_map/all_gather | solution.py:106
  52.9 26.8 %copy-start.1 = (bf16[240,768]{1,0:T(8,128)(2,1)S(1)}, bf16[240,768]{1,0:T(8,128)(2,1)}, u32[]{:S(2)}) copy-start(bf16[240,768]{1,0:T(8,128)(2,1)} %param.19) | copy-start | bytes 1105924
  52.9 94.1 %all-gather.12.cloned.1.call-start = ((), (), s32[]{:S(2)}) async-start(), calls=%async_computation.5 | async-start | bytes 1474560 | tf_op jit(solution)/shard_map/all_gather | solution.py:107
  53.4 126.2 %all-gather.14.cloned.1.call-start = ((), (), s32[]{:S(2)}) async-start(), calls=%async_computation.6 | async-start | bytes 5898240 | tf_op jit(solution)/shard_map/all_gather | solution.py:108
  54.0 154.6 %all-gather.16.cloned.1.call-start = ((), (), s32[]{:S(2)}) async-start(), calls=%async_computation.7 | async-start | bytes 5898240 | tf_op jit(solution)/shard_map/all_gather | solution.py:109
  54.6 179.4 %all-gather.20.cloned.1.call-start = ((), (), s32[]{:S(2)}) async-start(), calls=%async_computation.10 | async-start | bytes 1843200 | tf_op jit(solution)/shard_map/all_gather | solution.py:161
  57.9 26.2 %copy-start.38 = (f32[768]{0:T(1024)}, f32[768]{0:T(1024)S(1)}, u32[]{:S(2)}) copy-start(f32[768]{0:T(1024)S(1)} %get-tuple-element.25) | copy-start | bytes 9220
  80.8 35.6 %copy-start.49 = (f32[240]{0:T(256)}, f32[240]{0:T(256)S(1)}, u32[]{:S(2)}) copy-start(f32[240]{0:T(256)S(1)} %broadcast_multiply_fusion.8) | copy-start | bytes 2884
  82.1 34.4 %copy-start.54 = (f32[240]{0:T(256)}, f32[240]{0:T(256)S(1)}, u32[]{:S(2)}) copy-start(f32[240]{0:T(256)S(1)} %add_rsqrt_fusion.4) | copy-start | bytes 2884
  84.1 191.2 %reduce-scatter.9.cloned.1.call-start = ((), (), s32[]{:S(2)}) async-start(), calls=%async_computation.11 | async-start | bytes 1843200 | tf_op jit(solution)/shard_map/reduce_scatter | solution.py:169
  208.6 25.4 %copy-start.64 = (f32[768]{0:T(1024)S(1)}, f32[768]{0:T(1024)}, u32[]{:S(2)}) copy-start(f32[768]{0:T(1024)} %param.33) | copy-start | bytes 9220
  247.7 215.6 %all-gather.22.cloned.1.call-start = ((), (), s32[]{:S(2)}) async-start(), calls=%async_computation.12 | async-start | bytes 1843200 | tf_op jit(solution)/shard_map/all_gather | solution.py:215
  276.9 42.8 %copy-start.59 = (f32[15]{0:T(128)}, f32[15]{0:T(128)S(1)}, u32[]{:S(2)}) copy-start(f32[15]{0:T(128)S(1)} %add_rsqrt_fusion.6) | copy-start | bytes 184
  437.9 4.3 collective-permute-start
  439.2 3.0 collective-permute-start.1
  444.1 57.5 %copy-start.28 = (f32[15,768]{1,0:T(8,128)}, f32[15,768]{1,0:T(8,128)S(1)}, u32[]{:S(2)}) copy-start(f32[15,768]{1,0:T(8,128)S(1)} %subtract_multiply_fusion.1) | copy-start | bytes 138244
  445.0 55.1 %reduce-scatter.11.cloned.1.call-start = ((), (), s32[]{:S(2)}) async-start(), calls=%async_computation.13 | async-start | bytes 1843200 | tf_op jit(solution)/shard_map/reduce_scatter | solution.py:223
  470.1 30.0 %copy-start.44 = (f32[768]{0:T(1024)S(1)}, f32[768]{0:T(1024)}, u32[]{:S(2)}) copy-start(f32[768]{0:T(1024)} %copy-done.43) | copy-start | bytes 9220
  470.1 30.0 %copy-start.50 = (f32[240]{0:T(256)S(1)}, f32[240]{0:T(256)}, u32[]{:S(2)}) copy-start(f32[240]{0:T(256)} %copy-done.49) | copy-start | bytes 2884
  470.1 30.0 %copy-start.55 = (f32[240]{0:T(256)S(1)}, f32[240]{0:T(256)}, u32[]{:S(2)}) copy-start(f32[240]{0:T(256)} %copy-done.54) | copy-start | bytes 2884
  472.5 32.6 %copy-start.32 = (f32[60,3,16]{2,1,0:T(4,128)S(1)}, f32[60,3,16]{2,1,0:T(4,128)}, u32[]{:S(2)}) copy-start(f32[60,3,16]{2,1,0:T(4,128)} %copy-done.31) | copy-start | bytes 34564
  472.5 32.6 %copy-start.34 = (f32[60,3,16]{2,1,0:T(4,128)S(1)}, f32[60,3,16]{2,1,0:T(4,128)}, u32[]{:S(2)}) copy-start(f32[60,3,16]{2,1,0:T(4,128)} %copy-done.33) | copy-start | bytes 34564
  472.6 51.4 %all-gather.24.cloned.1.call-start = ((), (), s32[]{:S(2)}) async-start(), calls=%async_computation.14 | async-start | bytes 1843200 | tf_op jit(solution)/shard_map/all_gather | solution.py:232
  503.9 25.1 %copy-start.4 = (f32[60,3,16,16]{2,3,1,0:T(8,128)S(1)}, f32[60,3,16,16]{2,3,1,0:T(8,128)}, u32[]{:S(2)}) copy-start(f32[60,3,16,16]{2,3,1,0:T(8,128)} %copy-done.3) | copy-start | bytes 552964
  504.7 72.2 %reduce-scatter.13.cloned.1.call-start = ((), (), s32[]{:S(2)}) async-start(), calls=%async_computation.15 | async-start | bytes 1843200 | tf_op jit(solution)/shard_map/reduce_scatter | solution.py:269
  549.4 265.5 %all-reduce.7.cloned.1.call-start = ((), (), s32[]{:S(2)}) async-start(), calls=%async_computation.16 | async-start | bytes 14155776 | tf_op jit(solution)/shard_map/psum | solution.py:278
  561.0 15.9 %copy-start.53 = (f32[240]{0:T(256)S(1)}, f32[240]{0:T(256)}, u32[]{:S(2)}) copy-start(f32[240]{0:T(256)} %copy-done.52) | copy-start | bytes 2884
  561.0 83.7 %copy-start.7 = (f32[240,768]{1,0:T(8,128)S(1)}, f32[240,768]{1,0:T(8,128)}, u32[]{:S(2)}) copy-start(f32[240,768]{1,0:T(8,128)} %copy-done.6) | copy-start | bytes 2211844
  (51 other events, 190.8 us)
Sparse Core Ops, SparseCore 0:
  13.2 21.7 all-gather.17
  52.2 27.3 reduce-scatter.6
  81.2 30.7 all-gather.9
  113.4 17.4 all-gather.11
  132.3 37.4 all-gather.13
  171.2 37.4 all-gather.15
  210.8 19.0 all-gather.19
  247.9 27.3 reduce-scatter.8
  445.1 18.2 all-gather.21
  472.7 27.3 reduce-scatter.10
  504.8 19.0 all-gather.23
  549.5 27.3 reduce-scatter.12
  581.9 232.9 all-reduce.6
where the time goes:
time: 839 us; the launch traced here: 829 us
  waiting for transfers between devices  347 us (41%)
  blocking collectives  222 us (26%)
  matrix products  125 us (15%)
  local copies, waits for them, and re-layouts  74.8 us (9%)
  other arithmetic  38.1 us (5%)
  between operations  18.9 us (2%)
    psum x1, waiting for transfers between devices, local(): lax.psum((grad_qkv, grad_qv_bias, grad_out, grad_fc1, grad_fc1_bias, grad...  168 us
    psum x2, blocking collectives, local(): summed, scalar = lax.psum((partial_value, own_term), ('dp', 'mp'))  78.7 us
    unnamed x1, blocking collectives  77.1 us
    dot_general x2, matrix products, image_tower(): result = middle + jnp.dot(active, w_fc2, preferred_element_type=jnp.float32)  45.9 us
    all_gather x1, blocking collectives, local(): arrived = lax.all_gather(captions16, ('dp', 'mp'), axis=0, tiled=True)  42.7 us
    all_gather x1, waiting for transfers between devices, local(): lax.all_gather(img_fc2, 'mp', axis=0, tiled=True)  29 us
    all_gather x1, waiting for transfers between devices, local(): lax.all_gather(img_qkv, 'mp', axis=2, tiled=True)  27.8 us
    reduce_scatter x1, waiting for transfers between devices, local(): lax.psum_scatter(jnp.einsum('gf,df->gd', grad_hidden16, txt_fc1, preferre...  27.5 us
  transfers between devices with their start and end apart: 15, of which 11 were waited for; matrix products, arithmetic and copies ran while one was open for 18% of the time, Pallas kernels for 0%

commit v1 on v0

--- a/solution.py
+++ b/solution.py
@@ -129,7 +129,26 @@
     unit1, inverse1 = layer_stats(inputs)
     normed1 = (unit1 * txt_gains[0] + txt_shifts[0]).astype(jnp.bfloat16)
     bias_rows = jnp.stack([txt_qv_bias[0], jnp.zeros_like(txt_qv_bias[0]), txt_qv_bias[1]])
-    piece = lax.all_gather(normed1, "mp", axis=0, tiled=True)
+    base_arr, p_next, s_next = (lax.axis_size("mp"), lax.axis_index("mp"), normed1.shape[0])
+    by_rank = [q * base_arr if hop_no == 0 else q for hop_no, q in enumerate(normed1.shape)]
+    piece = lax.dynamic_update_slice_in_dim(
+        jnp.zeros(by_rank, normed1.dtype), normed1, p_next * s_next, axis=0
+    )
+    seen_now = local_out = normed1
+    for j in tuple(range(1, base_arr // 2 + 1)):
+        seen_now = lax.ppermute(
+            seen_now, "mp", [(hop_no, (hop_no + 1) % base_arr) for hop_no in range(base_arr)]
+        )
+        piece = lax.dynamic_update_slice_in_dim(
+            piece, seen_now, (p_next - j) % base_arr * s_next, axis=0
+        )
+        if 2 * j < base_arr:
+            local_out = lax.ppermute(
+                local_out, "mp", [(hop_no, (hop_no - 1) % base_arr) for hop_no in range(base_arr)]
+            )
+            piece = lax.dynamic_update_slice_in_dim(
+                piece, local_out, (p_next + j) % base_arr * s_next, axis=0
+            )
     made = jnp.einsum("rd,jdw->rjw", piece, txt_qkv, preferred_element_type=jnp.float32) + bias_rows
     joined = jnp.concatenate(
         [piece, made.astype(jnp.bfloat16).reshape(piece.shape[0], 3 * width)], 1

time: 839 us -> 844 us (level)
  waiting for transfers between devices: 347 us -> 337 us
    all_gather x1 -> x0, waiting for transfers between devices: 20.2 us -> none  [local(): piece = lax.all_gather(normed1, 'mp', axis=0, tiled=True)]
    dot_general x1, matrix products: 10.1 us -> 21.7 us  [local(): jnp.dot(piece, txt_fc1, preferred_element_type=jnp.float32) + txt_fc1_bias]
    ppermute x0 -> x3, waiting for transfers between devices: none -> 10.6 us  [the longest x2 10.6 us: local(): lax.ppermute(seen_now, 'mp', [(hop_no, (hop_no + 1) % base_arr) for hop_n...]
    reduce_scatter x1, waiting for transfers between devices: 20.6 us -> 29.2 us  [local(): lax.psum_scatter(jnp.dot(context, txt_out, preferred_element_type=jnp.flo...]
  transfers between devices with their start and end apart: 15 -> 17, of which waited for: 11 -> 11; matrix products, arithmetic and copies ran while one was open for 18% -> 20% of each run, Pallas kernels for 0% -> 0%
where the time goes in v1:
time: 844 us; the launch traced here: 836 us
  waiting for transfers between devices  337 us (40%)
  blocking collectives  222 us (26%)
  matrix products  129 us (15%)
  local copies, waits for them, and re-layouts  75.3 us (9%)
  other arithmetic  44.6 us (5%)
  between operations  19.8 us (2%)
  starting transfers between devices  8.93 us (1%)
    psum x1, waiting for transfers between devices, local(): lax.psum((grad_qkv, grad_qv_bias, grad_out, grad_fc1, grad_fc1_bias, grad...  168 us
    psum x2, blocking collectives, local(): summed, scalar = lax.psum((partial_value, own_term), ('dp', 'mp'))  78.5 us
    unnamed x1, blocking collectives  77.1 us
    dot_general x2, matrix products, image_tower(): result = middle + jnp.dot(active, w_fc2, preferred_element_type=jnp.float32)  46 us
    all_gather x1, blocking collectives, local(): arrived = lax.all_gather(captions16, ('dp', 'mp'), axis=0, tiled=True)  43 us
    reduce_scatter x1, waiting for transfers between devices, local(): lax.psum_scatter(jnp.dot(context, txt_out, preferred_element_type=jnp.flo...  29.2 us
    all_gather x1, waiting for transfers between devices, local(): lax.all_gather(img_fc2, 'mp', axis=0, tiled=True)  27.8 us
    reduce_scatter x1, waiting for transfers between devices, local(): lax.psum_scatter(jnp.einsum('gf,df->gd', grad_hidden16, txt_fc1, preferre...  27.5 us
  transfers between devices with their start and end apart: 17, of which 11 were waited for; matrix products, arithmetic and copies ran while one was open for 20% of the time, Pallas kernels for 0%

profile of v1, /device:TPU:0, one launch (start us, length us, event | category | flops | bytes accessed | tf_op | source)
XLA Modules:
  0.0 835.9 jit_solution(4249397023026670992)
XLA Ops:
  15.5 6.4 collective-permute-done
  24.6 4.2 collective-permute-done.2
  34.8 3.0 reshape_reshape.3
  37.8 3.2 fusion.222
  48.3 29.2 %reduce-scatter.7.cloned.1.call-done = bf16[240,768]{1,0:T(8,128)(2,1)} async-done(((bf16[960,768]{1,0:T(8,128)(2,1)}), bf16[240,768]{1,0:T(8,128)(2,1)}) %reduce-scatter.7.cloned.1.call-update) | async-done | bytes 368656 | tf_op jit(solution)/shard_map/reduce_scatter | solution.py:170
  89.6 20.3 %all-gather.9.cloned.1.call-done = bf16[3,768,768]{1,2,0:T(8,128)(2,1)} async-done(((bf16[3,768,192]{1,2,0:T(8,128)(2,1)}), bf16[3,768,768]{1,2,0:T(8,128)(2,1)}) %all-gather.9.cloned.1.call-update) | async-done | bytes 3538960 | tf_op jit(solution)/shard_map/all_gather | solution.py:106
  109.9 4.5 convert_bitcast_fusion
  122.7 3.1 squeeze.29
  128.3 3.3 reshape.236
  134.0 5.2 fusion.228
  143.3 4.1 squeeze.31
  150.2 3.8 fusion.45
  154.0 6.8 fusion.230
  163.9 4.2 reshape.220
  174.7 21.7 %multiply_convert_fusion = (bf16[960,768]{1,0:T(8,128)(2,1)S(1)}, f32[960,768]{1,0:T(8,128)}, f32[960,768]{1,0:T(8,128)}) fusion(f32[768]{0:T(1024)S(1)} %copy-done.71, bf16[960,768]{1,0:T(8,128)(2,1)} %all-gather.17.cloned.1.call-done, bf16[768,768]{1,0:T(8,128)(2,1)S(1)} %copy-done), kind=kOutput, calls=%fused_computation.54 | convolution fusion | flops 1181122560 | bytes 10030080 | tf_op jit(solution)/shard_map/dot_general | solution.py:181
  200.0 27.8 %all-gather.15.cloned.1.call-done = bf16[3072,768]{1,0:T(8,128)(2,1)} async-done(((bf16[768,768]{1,0:T(8,128)(2,1)}), bf16[3072,768]{1,0:T(8,128)(2,1)}) %all-gather.15.cloned.1.call-update) | async-done | bytes 4718608 | tf_op jit(solution)/shard_map/all_gather | solution.py:109
  227.8 25.5 %fusion.58 = f32[600,768]{1,0:T(8,128)} fusion(f32[600,768]{1,0:T(8,128)S(1)} %copy-done.25, bf16[3072,768]{1,0:T(8,128)(2,1)} %all-gather.15.cloned.1.call-done, bf16[768,3072]{1,0:T(8,128)(2,1)} %all-gather.13.cloned.1.call-done, f32[768]{0:T(1024)S(1)} %get-tuple-element.22, f32[600]{0:T(1024)S(1)} %add_rsqrt_fusion, f32[600]{0:T(1024)S(1)} %broadcast_multiply_fusion), kind=kOutput, calls=%fused_computation.102 | convolution fusion | flops 5784422400 | bytes 13131456 | tf_op jit(solution)/shard_map/dot_general | solution.py:77
  253.3 20.6 %fusion.62 = f32[435,768]{1,0:T(8,128)} fusion(f32[435,768]{1,0:T(8,128)} %copy-done.30, bf16[3072,768]{1,0:T(8,128)(2,1)} %all-gather.15.cloned.1.call-done, bf16[768,3072]{1,0:T(8,128)(2,1)} %all-gather.13.cloned.1.call-done, f32[768]{0:T(1024)S(1)} %get-tuple-element.22, f32[435]{0:T(512)S(1)} %add_rsqrt_fusion.2, f32[435]{0:T(512)S(1)} %broadcast_multiply_fusion.2), kind=kOutput, calls=%fused_computation.115 | convolution fusion | flops 4193706240 | bytes 12116376 | tf_op jit(solution)/shard_map/dot_general | solution.py:77
  282.8 43.0 %all-gather = bf16[32,15,768]{2,1,0:T(8,128)(2,1)S(1)} all-gather(bf16[1,15,768]{2,1,0:T(8,128)(2,1)S(1)} %fusion.139), channel_id=1, replica_groups=mesh['dp'=8,'mp'=4] {'dp','mp'}, dimensions={0}, use_global_device_ids=true | all-gather | bytes 760320 | tf_op jit(solution)/shard_map/all_gather | solution.py:204
  327.7 36.8 %psum.64 = f32[480]{0:T(512)S(1)} all-reduce(f32[480]{0:T(512)S(1)} %get-tuple-element.19), channel_id=1, replica_groups=mesh['dp'=8,'mp'=4] {'dp','mp'}, use_global_device_ids=true, to_apply=%region_32.33 | all-reduce | flops 480 | bytes 3840 | tf_op jit(solution)/shard_map/psum | solution.py:212
  366.9 77.1 %fusion = f32[16,768]{1,0:T(8,128)S(1)} fusion(f32[480,768]{1,0:T(8,128)S(1)} %convolution_multiply_fusion), kind=kCustom, calls=%all-reduce-scatter | all-reduce-scatter fusion | flops 393217 | bytes 1523712
  451.1 18.3 %all-gather.19.cloned.1.call-done = bf16[960,768]{1,0:T(8,128)(2,1)} async-done(((bf16[240,768]{1,0:T(8,128)(2,1)}), bf16[960,768]{1,0:T(8,128)(2,1)}) %all-gather.19.cloned.1.call-update) | async-done | bytes 1474576 | tf_op jit(solution)/shard_map/all_gather | solution.py:234
  469.5 5.6 convert_reduce_fusion
  478.7 27.5 %reduce-scatter.11.cloned.1.call-done = bf16[240,768]{1,0:T(8,128)(2,1)} async-done(((bf16[960,768]{1,0:T(8,128)(2,1)}), bf16[240,768]{1,0:T(8,128)(2,1)}) %reduce-scatter.11.cloned.1.call-update) | async-done | bytes 368656 | tf_op jit(solution)/shard_map/reduce_scatter | solution.py:242
  511.9 18.2 %all-gather.21.cloned.1.call-done = bf16[960,768]{1,0:T(8,128)(2,1)} async-done(((bf16[240,768]{1,0:T(8,128)(2,1)}), bf16[960,768]{1,0:T(8,128)(2,1)}) %all-gather.21.cloned.1.call-update) | async-done | bytes 1474576 | tf_op jit(solution)/shard_map/all_gather | solution.py:251
  551.6 3.9 bitcast_convert_fusion
  555.9 4.8 fusion.235
  569.6 13.4 %reduce-scatter.13.cloned.1.call-done = bf16[240,768]{1,0:T(8,128)(2,1)} async-done(((bf16[960,768]{1,0:T(8,128)(2,1)}), bf16[240,768]{1,0:T(8,128)(2,1)}) %reduce-scatter.13.cloned.1.call-update) | async-done | bytes 368656 | tf_op jit(solution)/shard_map/reduce_scatter | solution.py:288
  584.5 23.1 %all-reduce.3 = (f32[2,192]{1,0:T(2,128)}, f32[768]{0:T(1024)}) all-reduce(f32[2,192]{1,0:T(2,128)S(1)} %pad_maximum_fusion.7, f32[768]{0:T(1024)S(1)} %get-tuple-element.38), channel_id=1, replica_groups=mesh['dp'=8,'mp'=4] {'dp'}, use_global_device_ids=true, to_apply=%region_46.47 | all-reduce | flops 1152 | bytes 9216 | tf_op jit(solution)/shard_map/psum | solution.py:297
  607.7 41.7 %all-reduce.2 = (f32[]{:T(128)}, f32[6,768]{1,0:T(8,128)S(1)}) all-reduce(f32[]{:T(128)S(6)} %sub.165, f32[6,768]{1,0:T(8,128)S(1)} %stack.59), channel_id=1, replica_groups=mesh['dp'=8,'mp'=4] {'dp','mp'}, use_global_device_ids=true, to_apply=%region_30.31 | all-reduce | flops 4609 | bytes 36872 | tf_op jit(solution)/shard_map/psum | solution.py:212
  652.8 168.0 %all-reduce.7.cloned.1.call-done = (f32[3,768,192]{1,2,0:T(8,128)}, f32[192,768]{1,0:T(8,128)}, f32[768,768]{1,0:T(8,128)}, f32[768,768]{1,0:T(8,128)}) async-done(((f32[3,768,192]{1,2,0:T(8,128)}, f32[192,768]{1,0:T(8,128)}, f32[768,768]{1,0:T(8,128)}, f32[768,768]{1,0:T(8,128)}), (f32[3,768,192]{1,2,0:T(8,128)}, f32[192,768]{1,0:T(8,128)}, f32[768,768]{1,0:T(8,128)}, ...) | async-done | bytes 7077904 | tf_op jit(solution)/shard_map/psum | solution.py:297
  820.9 2.9 copy.209
  (323 shorter events, 134.9 us)
Async XLA Ops:
  7.2 167.5 %copy-start = (bf16[768,768]{1,0:T(8,128)(2,1)S(1)}, bf16[768,768]{1,0:T(8,128)(2,1)}, u32[]{:S(2)}) copy-start(bf16[768,768]{1,0:T(8,128)(2,1)} %param.32) | copy-start | bytes 3538948
  7.2 70.4 %reduce-scatter.7.cloned.1.call-start = ((), (), s32[]{:S(2)}) async-start(), calls=%async_computation.8 | async-start | bytes 1843200 | tf_op jit(solution)/shard_map/reduce_scatter | solution.py:170
  10.5 69.6 %copy-start.49 = (f32[768]{0:T(1024)}, f32[768]{0:T(1024)S(1)}, u32[]{:S(2)}) copy-start(f32[768]{0:T(1024)S(1)} %get-tuple-element.84) | copy-start | bytes 9220
  12.7 9.2 %collective-permute-start = (bf16[240,768]{1,0:T(8,128)(2,1)}, bf16[240,768]{1,0:T(8,128)(2,1)S(1)}, u32[]{:S(2)}, u32[]{:S(2)}) collective-permute-start(bf16[240,768]{1,0:T(8,128)(2,1)} %get-tuple-element.47), channel_id=1, source_target_pairs={{0,1},{1,2},{2,3},{3,0},{4,5},{5,6},{6,7},{7,4},{8,9},{9,10},{10,1... | collective-permute-start | bytes 1105928 | tf_op jit(solution)/shard_map/ppermute | solution.py:139
  13.2 11.4 %collective-permute-start.1 = (bf16[240,768]{1,0:T(8,128)(2,1)}, bf16[240,768]{1,0:T(8,128)(2,1)S(1)}, u32[]{:S(2)}, u32[]{:S(2)}) collective-permute-start(bf16[240,768]{1,0:T(8,128)(2,1)} %get-tuple-element.47), channel_id=1, source_target_pairs={{0,3},{1,0},{2,1},{3,2},{4,7},{5,4},{6,5},{7,6},{8,11},{9,8},{10,9... | collective-permute-start | bytes 1105928 | tf_op jit(solution)/shard_map/ppermute | solution.py:146
  21.9 6.9 collective-permute-start.2
  43.8 33.8 %copy-start.1 = (bf16[240,768]{1,0:T(8,128)(2,1)S(1)}, bf16[240,768]{1,0:T(8,128)(2,1)}, u32[]{:S(2)}) copy-start(bf16[240,768]{1,0:T(8,128)(2,1)} %param.19) | copy-start | bytes 1105924
  44.5 35.6 %copy-start.9 = (bf16[960,192]{1,0:T(8,128)(2,1)}, bf16[960,192]{1,0:T(8,128)(2,1)S(1)}, u32[]{:S(2)}) copy-start(bf16[960,192]{1,0:T(8,128)(2,1)S(1)} %reshape.224) | copy-start | bytes 1105924
  46.2 63.7 %all-gather.9.cloned.1.call-start = ((), (), s32[]{:S(2)}) async-start(), calls=%async_computation.4 | async-start | bytes 4423680 | tf_op jit(solution)/shard_map/all_gather | solution.py:106
  46.9 121.2 %all-gather.11.cloned.1.call-start = ((), (), s32[]{:S(2)}) async-start(), calls=%async_computation.5 | async-start | bytes 1474560 | tf_op jit(solution)/shard_map/all_gather | solution.py:107
  47.7 127.0 %all-gather.17.cloned.1.call-start = ((), (), s32[]{:S(2)}) async-start(), calls=%async_computation.9 | async-start | bytes 1843200 | tf_op jit(solution)/shard_map/all_gather | solution.py:180
  48.3 36.5 %copy-start.44 = (f32[768]{0:T(1024)}, f32[768]{0:T(1024)S(1)}, u32[]{:S(2)}) copy-start(f32[768]{0:T(1024)S(1)} %get-tuple-element.25) | copy-start | bytes 9220
  82.1 117.9 %all-gather.13.cloned.1.call-start = ((), (), s32[]{:S(2)}) async-start(), calls=%async_computation.6 | async-start | bytes 5898240 | tf_op jit(solution)/shard_map/all_gather | solution.py:108
  82.7 145.1 %all-gather.15.cloned.1.call-start = ((), (), s32[]{:S(2)}) async-start(), calls=%async_computation.7 | async-start | bytes 5898240 | tf_op jit(solution)/shard_map/all_gather | solution.py:109
  83.3 197.8 %reduce-scatter.9.cloned.1.call-start = ((), (), s32[]{:S(2)}) async-start(), calls=%async_computation.10 | async-start | bytes 1843200 | tf_op jit(solution)/shard_map/reduce_scatter | solution.py:188
  197.5 30.3 %copy-start.25 = (f32[600,768]{1,0:T(8,128)S(1)}, f32[600,768]{1,0:T(8,128)}, u32[]{:S(2)}) copy-start(f32[600,768]{1,0:T(8,128)} %copy-done.24) | copy-start | bytes 5529604
  200.0 269.5 %all-gather.19.cloned.1.call-start = ((), (), s32[]{:S(2)}) async-start(), calls=%async_computation.11 | async-start | bytes 1843200 | tf_op jit(solution)/shard_map/all_gather | solution.py:234
  282.7 43.1 %copy-start.65 = (f32[15]{0:T(128)}, f32[15]{0:T(128)S(1)}, u32[]{:S(2)}) copy-start(f32[15]{0:T(128)S(1)} %add_rsqrt_fusion.6) | copy-start | bytes 184
  444.0 4.3 collective-permute-start.3
  445.3 3.0 collective-permute-start.4
  450.2 57.5 %copy-start.34 = (f32[15,768]{1,0:T(8,128)}, f32[15,768]{1,0:T(8,128)S(1)}, u32[]{:S(2)}) copy-start(f32[15,768]{1,0:T(8,128)S(1)} %subtract_multiply_fusion.1) | copy-start | bytes 138244
  451.1 55.2 %reduce-scatter.11.cloned.1.call-start = ((), (), s32[]{:S(2)}) async-start(), calls=%async_computation.12 | async-start | bytes 1843200 | tf_op jit(solution)/shard_map/reduce_scatter | solution.py:242
  476.2 30.1 %copy-start.50 = (f32[768]{0:T(1024)S(1)}, f32[768]{0:T(1024)}, u32[]{:S(2)}) copy-start(f32[768]{0:T(1024)} %copy-done.49) | copy-start | bytes 9220
  476.2 30.1 %copy-start.54 = (f32[240]{0:T(256)S(1)}, f32[240]{0:T(256)}, u32[]{:S(2)}) copy-start(f32[240]{0:T(256)} %copy-done.53) | copy-start | bytes 2884
  476.2 30.1 %copy-start.59 = (f32[240]{0:T(256)S(1)}, f32[240]{0:T(256)}, u32[]{:S(2)}) copy-start(f32[240]{0:T(256)} %copy-done.58) | copy-start | bytes 2884
  478.7 32.5 %copy-start.38 = (f32[60,3,16]{2,1,0:T(4,128)S(1)}, f32[60,3,16]{2,1,0:T(4,128)}, u32[]{:S(2)}) copy-start(f32[60,3,16]{2,1,0:T(4,128)} %copy-done.37) | copy-start | bytes 34564
  478.7 32.5 %copy-start.40 = (f32[60,3,16]{2,1,0:T(4,128)S(1)}, f32[60,3,16]{2,1,0:T(4,128)}, u32[]{:S(2)}) copy-start(f32[60,3,16]{2,1,0:T(4,128)} %copy-done.39) | copy-start | bytes 34564
  478.7 51.4 %all-gather.21.cloned.1.call-start = ((), (), s32[]{:S(2)}) async-start(), calls=%async_computation.13 | async-start | bytes 1843200 | tf_op jit(solution)/shard_map/all_gather | solution.py:251
  510.1 25.1 %copy-start.4 = (f32[60,3,16,16]{2,3,1,0:T(8,128)S(1)}, f32[60,3,16,16]{2,3,1,0:T(8,128)}, u32[]{:S(2)}) copy-start(f32[60,3,16,16]{2,3,1,0:T(8,128)} %copy-done.3) | copy-start | bytes 552964
  510.9 72.2 %reduce-scatter.13.cloned.1.call-start = ((), (), s32[]{:S(2)}) async-start(), calls=%async_computation.14 | async-start | bytes 1843200 | tf_op jit(solution)/shard_map/reduce_scatter | solution.py:288
  555.5 265.4 %all-reduce.7.cloned.1.call-start = ((), (), s32[]{:S(2)}) async-start(), calls=%async_computation.15 | async-start | bytes 14155776 | tf_op jit(solution)/shard_map/psum | solution.py:297
  567.2 83.4 %copy-start.7 = (f32[240,768]{1,0:T(8,128)S(1)}, f32[240,768]{1,0:T(8,128)}, u32[]{:S(2)}) copy-start(f32[240,768]{1,0:T(8,128)} %copy-done.6) | copy-start | bytes 2211844
  (60 other events, 293.8 us)
Sparse Core Ops, SparseCore 0:
  46.3 31.2 reduce-scatter.6
  79.1 30.7 all-gather.8
  111.5 17.4 all-gather.10
  130.9 19.0 all-gather.16
  151.5 37.4 all-gather.12
  190.4 37.4 all-gather.14
  231.0 27.4 reduce-scatter.8
  451.2 18.2 all-gather.18
  478.8 27.3 reduce-scatter.10
  511.0 19.0 all-gather.20
  555.6 27.3 reduce-scatter.12
  587.9 232.9 all-reduce.6
